TPU v7x, 32 devices: a whole 2x2x4 slice. The times are simulated.
32 devices in a mesh: qrow: 4 (over y, x), kcol: 8 (over z, core).
Axes of the slice: x: 2, y: 2, z: 4, core: 2. Of those that a mesh axis runs over, the one named last changes fastest.
Arguments:
- queries: bfloat16 [8192, 512], P(('qrow', 'kcol')), may hold values from -6 to 6
- keys: bfloat16 [8192, 128], P(('kcol', 'qrow')), may hold values from -6 to 6
- values: bfloat16 [8192, 128], P(('kcol', 'qrow')), may hold values from -6 to 6
- block_mask: int32 [64, 64], replicated, may hold values from 0 to 1, as said below
Outputs:
- attended: float32 [8192, 512], P(('qrow', 'kcol'))
Inputs may be any that keep to these rules, and one draw needn't show every extreme that they name: block_mask[a, b] is 1 only where b <= a, and always where 0 <= a - b < 3.
All inputs are finite; a program needn't handle non-finite values.
Results may differ from a plain program's by a relative error of at most 0.0022.
Values may be sent and summed in bfloat16 or wider, within the bound.
A program may use at most 64 MiB of HBM per device.

v0:
```python
import functools
import math

import jax
import jax.numpy as jnp
from jax import lax
from jax.experimental import pallas as pl
from jax.experimental.pallas import tpu as pltpu
from jax.sharding import PartitionSpec as P

H = 4
DH = 128
BLOCK = 128
SIZES = (16, 8, 4)
NEAR = 3
TILE = 256
BIG = 4e30
MOST = 64
REACH = 1
HALVES = 1
SCAN = 16
NEG_FILL = -1e30
SCALE = math.log2(math.e) / math.sqrt(DH)


def columns_of(t):
    return slice(t * TILE, (t + 1) * TILE)


def prepare(q_ref, flipped, total, mass, top):
    tokens = q_ref.shape[0]
    part = min(tokens, BLOCK)
    width = H * part
    for own in range(tokens // part):
        turned = jnp.concatenate(
            [
                q_ref[own * part : (own + 1) * part, h * DH : (h + 1) * DH].T
                for h in range(H)
            ],
            axis=1,
        )
        scaled = turned.astype(jnp.float32) * SCALE
        coarse = scaled.astype(jnp.bfloat16)
        at = slice(own * width, (own + 1) * width)
        flipped[:DH, at] = coarse
        flipped[DH:, at] = (scaled - coarse.astype(jnp.float32)).astype(jnp.bfloat16)
    total[...] = jnp.zeros_like(total)
    mass[...] = jnp.zeros_like(mass)
    top[...] = jnp.full_like(top, NEG_FILL)


def operands(key_rows, value_rows):
    ones = jnp.ones((16, value_rows.shape[0]), jnp.bfloat16)
    return (
        jnp.concatenate([key_rows, key_rows], axis=1),
        jnp.concatenate([value_rows.T, ones], axis=0),
    )


def attend_to(state, lists, width, causal=None):
    flipped, total, mass, top = state
    tiles = flipped.shape[1] // TILE

    def scores_of(t):
        keys = lists[t * TILE // width][0]
        return jnp.dot(keys, flipped[:, columns_of(t)], preferred_element_type=jnp.float32)

    def weigh(t, scores):
        columns = columns_of(t)
        absent = lists[t * TILE // width][2]
        pieces = [scores[g * BLOCK : (g + 1) * BLOCK] for g in range(len(absent))]
        if causal is not None:
            pieces[0] = causal(t, pieces[0])
        old = top[:, columns]
        new = old
        for piece, off in zip(pieces, absent):
            new = jnp.maximum(new, jnp.max(piece, axis=0, keepdims=True) - off)
        top[:, columns] = new
        weights = [
            jnp.exp2(piece - (new + off)).astype(jnp.bfloat16)
            for piece, off in zip(pieces, absent)
        ]
        return jnp.exp2(old - new), jnp.concatenate(weights, axis=0)

    def gather(t, fade, weights):
        columns = columns_of(t)
        values = lists[t * TILE // width][1]
        summed = jnp.dot(values, weights, preferred_element_type=jnp.float32)
        mass[:, columns] = mass[:, columns] * fade + summed[DH : DH + 1]
        total[:, columns] = total[:, columns] * fade + summed[:DH]

    scores, held_back = scores_of(0), None
    for t in range(tiles):
        ahead = scores_of(t + 1) if t + 1 < tiles else None
        weighed = weigh(t, scores)
        if held_back is not None:
            gather(t - 1, *held_back)
        scores, held_back = ahead, weighed
    gather(tiles - 1, *held_back)


def penalty(here):
    return jnp.where(here, 0.0, BIG).astype(jnp.float32)


def absorbed(plane, q, z):
    spare = (plane < z) & (z + 1 < q)
    return (plane < q) & (plane - z <= REACH) & (z - plane <= REACH) & ~spare


def attend(
    early, mask_hbm, turned, old_total, old_mass, old_top, k_ref, v_ref, out_ref,
    mask_ref, listed, total, mass, top, held, sent, fetched,
):
    fetch = pltpu.make_async_copy(mask_hbm, mask_ref, fetched.at[0])
    fetch.start()
    tokens = out_ref.shape[0]
    part = min(tokens, BLOCK)
    pieces_here = tokens // part
    width = H * part
    last = mask_ref.shape[1] - 1
    q, c = lax.axis_index("qrow"), lax.axis_index("kcol")
    device = q * lax.axis_size("kcol") + c
    plane_blocks = 2 * lax.axis_size("qrow") * tokens // BLOCK
    firsts = [device * tokens + own * part for own in range(pieces_here)]
    rows = [first // BLOCK for first in firsts]
    state = (turned, total, mass, top)
    total[...] = old_total[...]
    mass[...] = old_mass[...]
    top[...] = old_top[...]

    def gone(block):
        if not early:
            return block < 0
        return absorbed(lax.div(block, plane_blocks), q, c // 2)

    def rows_of(ref, blocks):
        return jnp.concatenate(
            [ref[pl.ds(pl.multiple_of(b * BLOCK, BLOCK), BLOCK), :] for b in blocks], axis=0
        )

    def gathered_list(blocks, absent):
        keys, values = operands(rows_of(k_ref, blocks), rows_of(v_ref, blocks))
        return keys, values, absent

    def causal(t, piece):
        key_at = lax.broadcasted_iota(jnp.int32, piece.shape, 0)
        query_at = lax.broadcasted_iota(jnp.int32, piece.shape, 1) % part
        query_at = query_at + firsts[t * TILE // width] % BLOCK
        return jnp.where(key_at <= query_at, piece, -BIG)

    near = []
    for row in rows:
        blocks = [jnp.maximum(row - back, 0) for back in range(NEAR)]
        absent = [
            penalty((row >= back) & ~gone(block)) for back, block in enumerate(blocks)
        ]
        near.append(gathered_list(blocks, absent))
    attend_to(state, near, width, causal)

    fetch.wait()

    def scan(s, counts):
        lowest = last + 1 - (s + 1) * SCAN

        def note(_, counts):
            found = list(counts)
            for i in reversed(range(SCAN)):
                j = lowest + i
                for own, row in enumerate(rows):
                    listed[own, found[own]] = j
                    far = (j + NEAR <= row).astype(jnp.int32)
                    found[own] = found[own] + far * mask_ref[row, j]
            return tuple(found)

        skip = gone(lowest) | (lowest > rows[-1])
        return lax.fori_loop(0, jnp.where(skip, 0, 1), note, counts)

    counts = lax.fori_loop(
        0, (last + 1) // SCAN, scan, tuple(jnp.int32(0) for _ in rows)
    )
    most = counts[0]
    for count in counts[1:]:
        most = jnp.maximum(most, count)
    done = jnp.int32(0)
    for size in SIZES:
        left = most - done
        trips = left // size if size > SIZES[-1] else (left + size - 1) // size

        def step(t, carried, done=done, size=size):
            start = done + t * size
            lists = []
            for own, count in enumerate(counts):
                here = [start + g < count for g in range(size)]
                blocks = [
                    jnp.where(here[g], listed[own, jnp.minimum(start + g, last)], 0)
                    for g in range(size)
                ]
                lists.append(gathered_list(blocks, [penalty(ok) for ok in here]))
            attend_to(state, lists, width)
            return carried

        lax.fori_loop(0, trips, step, 0)
        done = done + trips * size

    copies = []
    for own in range(pieces_here):
        here = pl.ds(own * part, part)
        for h in range(H):
            at = slice(own * width + h * part, own * width + (h + 1) * part)
            held[here, h * DH : (h + 1) * DH] = (total[:, at] / mass[:, at]).T
        copy = pltpu.make_async_copy(held.at[here, :], out_ref.at[here, :], sent.at[own])
        copy.start()
        copies.append(copy)
    for copy in copies:
        copy.wait()


def spread(
    q_hbm, k_ref, v_ref, mask_hbm, k_all, v_all, flipped, total, mass, top,
    q_ref, mask_ref, send, recv, shared, local, fetched,
):
    ring, lane = lax.axis_size("kcol"), lax.axis_size("qrow")
    depth, width = ring // 2, lane // 2
    q, c = lax.axis_index("qrow"), lax.axis_index("kcol")
    level, core = c // 2, c % 2
    high, low = q // width, q % width
    tokens = k_ref.shape[0]
    own, whole = (k_ref, v_ref), (k_all, v_all)
    sibling = {"qrow": q, "kcol": level * 2 + (1 - core)}
    over = {"qrow": (1 - high) * width + low, "kcol": c}
    sides = [(low + i) % width for i in range(1, width)]
    beside = [{"qrow": high * width + i, "kcol": c} for i in sides]
    up = {"qrow": q, "kcol": c + 2}
    down = {"qrow": q, "kcol": c - 2}
    has_up, has_down = level < depth - 1, level > 0

    def slot(at, column, parity=core):
        return (at * 2 + parity) * lane + column

    def place(kv, block):
        return whole[kv].at[pl.ds(pl.multiple_of(block * tokens, tokens), tokens), :]

    copies = [
        pltpu.make_async_copy(own[kv], place(kv, slot(level, q)), local.at[kv]) for kv in range(2)
    ]
    for copy in copies:
        copy.start()

    fetches = [
        pltpu.make_async_copy(q_hbm, q_ref, fetched.at[0]),
        pltpu.make_async_copy(mask_hbm, mask_ref, fetched.at[1]),
    ]
    for fetch in fetches:
        fetch.start()

    barrier = pltpu.get_barrier_semaphore()

    def greet(target):
        pl.semaphore_signal(
            barrier, inc=1, device_id=target, device_id_type=pl.DeviceIdType.MESH
        )

    for target in [sibling, over] + beside:
        greet(target)
    pl.when(has_up)(lambda: greet(up))
    pl.when(has_down)(lambda: greet(down))
    ends = has_up.astype(jnp.int32) + has_down.astype(jnp.int32)
    pl.semaphore_wait(barrier, 2 + len(beside) + ends)

    for copy in copies:
        copy.wait()

    final = depth - 1
    mine = q == lane - 1
    over_last = (high == 0) & (low == width - 1)
    over_at, up_at, down_at = 1, 2, 2 + depth
    beside_at = 2 + 2 * depth
    relay_over_at = beside_at + len(beside)
    relay_beside_at = relay_over_at + 1
    lift_at = relay_beside_at + len(beside)
    spare_at = lift_at + 2
    end_over_at = spare_at + depth
    end_beside_at = end_over_at + 2
    end_relay_over_at = end_beside_at + 2 * len(beside)
    end_relay_beside_at = end_relay_over_at + 1

    def beside_last(i):
        return high * width + i == lane - 1

    def end_over(kv):
        return high == 0 if kv == 1 else over_last

    def end_beside(kv, i):
        return i == width - 1 if kv == 0 else beside_last(i)

    def settled(semaphore, rows):
        span = k_all.at[pl.ds(0, rows), :]
        pltpu.make_async_copy(span, span, semaphore).wait()

    def landed(kv, block):
        settled(recv.at[kv, block], tokens)

    def push(kv, block, target, at, arrival=None):
        pltpu.make_async_remote_copy(
            src_ref=place(kv, block),
            dst_ref=place(kv, block),
            send_sem=send.at[at],
            recv_sem=recv.at[kv, block] if arrival is None else arrival,
            device_id=target,
            device_id_type=pl.DeviceIdType.MESH,
        ).start()

    def to_sibling(kv, block, at):
        push(kv, block, sibling, 0, shared.at[at])

    def guarded(ok, body):
        if ok is None:
            body()
        else:
            pl.when(ok)(body)

    def lifted(at):
        return ((at == 0) & (level >= 2)) | ((at == depth - 1) & (level < depth - 2))

    def sent_where(at, way, conditions, body):
        if way <= 0:
            conditions = conditions[:1] + [(at != final) | conditions[1]]
        else:
            conditions = conditions[:1]
        conditions = [c for c in conditions if c is not None]
        if not conditions:
            body()
        else:
            ok = conditions[0]
            for c in conditions[1:]:
                ok &= c
            pl.when(ok)(body)

    def either(at, way, end, usual):
        return jnp.where(at == final, end, usual) if way <= 0 else usual

    def lift(kv, block, at, way):
        if way > 0:
            pl.when((at == 0) & has_up)(lambda: push(kv, block, up, lift_at))
        if way < 0:
            pl.when((at == depth - 1) & has_down)(lambda: push(kv, block, down, lift_at + 1))

    def column_sends(ok, at, way):
        block = slot(at, q)

        def body():
            for kv in range(2):
                if way != 0:
                    landed(kv, block)
                if way >= 0:
                    pl.when(has_up)(lambda: push(kv, block, up, up_at + at))
                if way <= 0:
                    pl.when(has_down)(lambda: push(kv, block, down, down_at + at))
                on_time = None if kv == 1 or way == 0 else ~lifted(at)
                usual = over_at if kv == 1 else spare_at + at
                sent_where(
                    at, way, [on_time, end_over(kv)],
                    lambda: push(kv, block, over, either(at, way, end_over_at + kv, usual)),
                )
                on_time = None if kv == 0 or way == 0 else ~lifted(at)
                for i, (column, target) in enumerate(zip(sides, beside)):
                    usual = beside_at + i if kv == 0 else spare_at + at
                    sent_where(
                        at, way, [on_time, end_beside(kv, column)],
                        lambda: push(
                            kv, block, target,
                            either(at, way, end_beside_at + 2 * i + kv, usual),
                        ),
                    )
                sent_where(at, way, [None, mine], lambda: to_sibling(kv, block, at))

        guarded(ok, body)

    def relays(ok, at, way):
        def body():
            def keys_over():
                for i in sides:
                    block = slot(at, high * width + i)
                    landed(0, block)
                    at_end = end_relay_over_at
                    sent_where(
                        at, way, [None, over_last],
                        lambda: push(0, block, over, either(at, way, at_end, relay_over_at)),
                    )
                    sent_where(at, way, [None, mine], lambda: to_sibling(0, block, at))

            def values_beside():
                block = slot(at, (1 - high) * width + low)
                landed(1, block)
                for i, (column, target) in enumerate(zip(sides, beside)):
                    at_end = end_relay_beside_at + i
                    sent_where(
                        at, way, [None, beside_last(column)],
                        lambda: push(
                            1, block, target, either(at, way, at_end, relay_beside_at + i)
                        ),
                    )
                sent_where(at, way, [None, mine], lambda: to_sibling(1, block, at))

            def rest():
                block = slot(at, (1 - high) * width + low)
                landed(0, block)
                lift(0, block, at, way)
                to_sibling(0, block, at)
                for i in sides:
                    block = slot(at, high * width + i)
                    landed(1, block)
                    lift(1, block, at, way)
                    to_sibling(1, block, at)

            sent_where(at, way, [None, low == width - 1], keys_over)
            sent_where(at, way, [None, high == 1], values_beside)
            sent_where(at, way, [None, mine], rest)

        guarded(ok, body)

    def corners(ok, at, way):
        def body():
            for i in sides:
                block = slot(at, (1 - high) * width + i)
                for kv in range(2):
                    landed(kv, block)
                    to_sibling(kv, block, at)

        if way <= 0:
            needed = (at != final) | mine
            ok = needed if ok is None else ok & needed
        guarded(ok, body)

    def positions(step):
        if step == 0:
            return [(None, level, 0)]
        return [
            (level >= step, level - step, 1),
            (level + step < depth, level + step, -1),
        ]

    state = (flipped, total, mass, top)
    part = min(q_ref.shape[0], BLOCK)
    firsts = [(q * ring + c) * q_ref.shape[0] + own for own in range(0, q_ref.shape[0], part)]
    plane_tokens = 2 * lane * tokens
    half_tokens = plane_tokens // HALVES

    def absorb(step):
        for ok, at, _ in positions(step):
            here = absorbed(at, q, level) if ok is None else ok & absorbed(at, q, level)
            pl.when(here)(lambda at=at: settled(shared.at[at], plane_tokens))

        def half(i, carried):
            plane = jnp.where(i < HALVES, level - step, level + step)
            first = plane * plane_tokens + i % HALVES * half_tokens
            here = pl.ds(pl.multiple_of(first, half_tokens), half_tokens)
            keys, values = operands(k_all[here, :], v_all[here, :])
            lists = []
            for token in firsts:
                absent = [
                    (1 - mask_ref[token // BLOCK, first // BLOCK + g]).astype(jnp.float32) * BIG
                    for g in range(half_tokens // BLOCK)
                ]
                lists.append((keys, values, absent))
            attend_to(state, lists, H * part)
            return carried

        below = (level >= step) & absorbed(level - step, q, level)
        above = (level + step < depth) & (level + step < q) & (step > 0)
        lax.fori_loop(
            jnp.where(below, 0, HALVES), jnp.where(above, 2 * HALVES, HALVES), half, 0
        )

    for step in range(depth + 2):
        if step < depth:
            for ok, at, way in positions(step):
                column_sends(ok, at, way)
        if step == 0:
            for fetch in fetches:
                fetch.wait()
            prepare(q_ref, flipped, total, mass, top)
        if 1 <= step <= depth:
            for ok, at, way in positions(step - 1):
                relays(ok, at, way)
        if step >= 2:
            for ok, at, way in positions(step - 2):
                corners(ok, at, way)
            if step - 2 <= REACH:
                absorb(step - 2)
    for at in range(depth):
        here = ~absorbed(at, q, level)
        if at == final:
            here &= mine
        pl.when(here)(lambda at=at: settled(shared.at[at], plane_tokens))
    pl.when(mine)(lambda: settled(send.at[0], depth * plane_tokens))
    pl.when(~mine)(lambda: settled(send.at[0], final * plane_tokens))
    settled(send.at[over_at], final * tokens)
    settled(send.at[relay_over_at], len(sides) * final * tokens)
    pl.when(over_last)(lambda: settled(send.at[end_relay_over_at], len(sides) * tokens))
    for i, column in enumerate(sides):
        settled(send.at[beside_at + i], final * tokens)
        settled(send.at[relay_beside_at + i], final * tokens)
        pl.when(beside_last(column))(
            lambda i=i: settled(send.at[end_relay_beside_at + i], tokens)
        )
    for kv in range(2):
        on_time = ~lifted(final)
        late = end_over(kv) & on_time if kv == 0 else end_over(kv)
        pl.when(late)(lambda kv=kv: settled(send.at[end_over_at + kv], tokens))
        for i, column in enumerate(sides):
            late = end_beside(kv, column) & on_time if kv == 1 else end_beside(kv, column)
            pl.when(late)(
                lambda i=i, kv=kv: settled(send.at[end_beside_at + 2 * i + kv], tokens)
            )
    lifts = (len(sides) + 1) * tokens
    pl.when(has_up & (level > 0))(lambda: settled(send.at[lift_at], lifts))
    pl.when(has_down & (level < final) & mine)(
        lambda: settled(send.at[lift_at + 1], lifts)
    )
    for at in range(final):
        pl.when(~lifted(at))(
            lambda at=at: settled(send.at[spare_at + at], (1 + len(beside)) * tokens)
        )
    for at in range(depth):
        pl.when(has_up & (level >= at))(lambda at=at: settled(send.at[up_at + at], 2 * tokens))
        pl.when(has_down & (level <= at))(
            lambda at=at: settled(send.at[down_at + at], 2 * tokens)
        )


def in_hbm(array):
    return pltpu.with_memory_space_constraint(array, pltpu.HBM)


def state_of(queries):
    columns = queries.shape[0] * H
    row = jax.ShapeDtypeStruct((1, columns), jnp.float32)
    return (
        jax.ShapeDtypeStruct((2 * DH, columns), jnp.bfloat16),
        jax.ShapeDtypeStruct((DH, columns), jnp.float32),
        row,
        row,
    )


def gathered(queries, keys, values, block_mask):
    ring, lane = lax.axis_size("kcol"), lax.axis_size("qrow")
    devices = ring * lane
    vmem = pl.BlockSpec(memory_space=pltpu.VMEM)
    state = state_of(queries)
    if ring != 2 * lane or lane % 2 or devices > MOST:
        both = ("kcol", "qrow")
        ready = pl.pallas_call(
            prepare, out_shape=state, in_specs=[vmem], out_specs=(vmem,) * len(state)
        )(queries)
        return False, ready, (
            lax.all_gather(keys, both, axis=0, tiled=True),
            lax.all_gather(values, both, axis=0, tiled=True),
        )
    full = jax.ShapeDtypeStruct((keys.shape[0] * devices, keys.shape[1]), keys.dtype)
    side = lane // 2 - 1
    all_keys, all_values, *ready = pl.pallas_call(
        spread,
        out_shape=(full, full) + state,
        in_specs=[pl.BlockSpec(memory_space=pltpu.HBM)] * 4,
        out_specs=(vmem,) * (2 + len(state)),
        scratch_shapes=[
            pltpu.VMEM(queries.shape, queries.dtype),
            pltpu.SMEM(block_mask.shape, jnp.int32),
            pltpu.SemaphoreType.DMA((8 + ring + ring // 2 + 5 * side,)),
            pltpu.SemaphoreType.DMA((2, devices)),
            pltpu.SemaphoreType.DMA((ring // 2,)),
            pltpu.SemaphoreType.DMA((2,)),
            pltpu.SemaphoreType.DMA((2,)),
        ],
        compiler_params=pltpu.CompilerParams(
            collective_id=0, has_side_effects=True, vmem_limit_bytes=40 * 2**20
        ),
    )(in_hbm(queries), in_hbm(keys), in_hbm(values), in_hbm(block_mask))
    return True, ready, (all_keys, all_values)


def shards(queries, keys, values, block_mask):
    early, ready, everything = gathered(queries, keys, values, block_mask)
    vmem = pl.BlockSpec(memory_space=pltpu.VMEM)
    hbm = pl.BlockSpec(memory_space=pltpu.HBM)
    _, *sums = state_of(queries)
    parts = pl.cdiv(queries.shape[0], BLOCK)
    return pl.pallas_call(
        functools.partial(attend, early),
        out_shape=jax.ShapeDtypeStruct(queries.shape, jnp.float32),
        in_specs=[hbm] + [vmem] * 6,
        out_specs=hbm,
        scratch_shapes=[
            pltpu.SMEM(block_mask.shape, jnp.int32),
            pltpu.SMEM((parts, block_mask.shape[1]), jnp.int32),
            *[pltpu.VMEM(s.shape, s.dtype) for s in sums],
            pltpu.VMEM(queries.shape, jnp.float32),
            pltpu.SemaphoreType.DMA((parts,)),
            pltpu.SemaphoreType.DMA((1,)),
        ],
        compiler_params=pltpu.CompilerParams(vmem_limit_bytes=48 * 2**20),
    )(in_hbm(block_mask), *ready, *everything)


def solution(mesh):
    placed = (P(("qrow", "kcol"), None), P(("kcol", "qrow"), None), P(("kcol", "qrow"), None), P())
    return jax.shard_map(
        shards, mesh=mesh, in_specs=placed, out_specs=P(("qrow", "kcol"), None), check_vma=False
    )
```

profile of v0, /device:TPU:29, one launch (start us, length us, event | category | flops | bytes accessed | tf_op | source)
XLA Modules:
  0.0 30.1 jit_solution(3503268032419835125)
XLA Ops:
  0.0 23.8 %shard_map.46 = (bf16[8192,128]{1,0:T(8,128)(2,1)S(1)}, bf16[8192,128]{1,0:T(8,128)(2,1)S(1)}, bf16[256,1024]{1,0:T(8,128)(2,1)S(1)}, f32[128,1024]{1,0:T(8,128)...) custom-call(bf16[256,512]{1,0:T(8,128)(2,1)} %q_hbm.1, bf16[256,128]{1,0:T(8,128)(2,1)} %k_ref.1, ...), custom_call_target="tpu_custom_call" | custom-call | tf_op jit(solution)/shard_map/pallas_call | solution.py:564
  23.8 6.3 %shard_map.47 = f32[256,512]{1,0:T(8,128)} custom-call(s32[64,64]{1,0:T(8,128)} %mask_hbm.3, bf16[256,1024]{1,0:T(8,128)(2,1)S(1)} %get-tuple-element.11.turned, f32[128,1024]{1,0:T(8,128)S(1)} %get-tuple-element.12.old_total, f32[1,1024]{1,0:T(1,128)S(1)} %get-tuple-element.13.old_mass, f32[1,1024]{1,0:T(1,128)S(1)} %get-tuple-element.14.old_top, ...), custom_call_target="tpu_custom_call" | custom-call | tf_op jit(solution)/shard_map/pallas_call | solution.py:591
where the time goes:
time: 30.4 us; the launch traced here: 30.1 us
  Pallas kernels  30.1 us (99%)
    pallas_call x1, Pallas kernels, gathered(): pl.pallas_call(spread, out_shape=(full, full) + state, in_specs=[pl.Block...  23.8 us
    pallas_call x1, Pallas kernels, shards(): pl.pallas_call(functools.partial(attend, early), out_shape=jax.ShapeDtype...  6.27 us

commit v1 on v0

--- a/solution.py
+++ b/solution.py
@@ -11,7 +11,7 @@
 H = 4
 DH = 128
 BLOCK = 128
-SIZES = (16, 8, 4)
+SIZES = (20, 12, 4)
 NEAR = 3
 TILE = 256
 BIG = 4e30
@@ -183,9 +183,9 @@
     for count in counts[1:]:
         most = jnp.maximum(most, count)
     done = jnp.int32(0)
-    for size in SIZES:
+    for size, smaller in zip(SIZES, SIZES[1:] + (0,)):
         left = most - done
-        trips = left // size if size > SIZES[-1] else (left + size - 1) // size
+        trips = jnp.where(left > smaller, (left + size - smaller - 1) // size, 0)
 
         def step(t, carried, done=done, size=size):
             start = done + t * size

time: 30.4 us -> 30 us (0.987)
  Pallas kernels: 30.1 us -> 29.5 us
    pallas_call x1, Pallas kernels: 6.27 us -> 5.67 us  [shards(): pl.pallas_call(functools.partial(attend, early), out_shape=jax.ShapeDtype...]
where the time goes in v1:
time: 30 us; the launch traced here: 29.5 us
  Pallas kernels  29.5 us (98%)
    pallas_call x1, Pallas kernels, gathered(): pl.pallas_call(spread, out_shape=(full, full) + state, in_specs=[pl.Block...  23.8 us
    pallas_call x1, Pallas kernels, shards(): pl.pallas_call(functools.partial(attend, early), out_shape=jax.ShapeDtype...  5.67 us

profile of v1, /device:TPU:29, one launch (start us, length us, event | category | flops | bytes accessed | tf_op | source)
XLA Modules:
  0.0 29.5 jit_solution(4343457929177531462)
XLA Ops:
  0.0 23.8 %shard_map.46 = (bf16[8192,128]{1,0:T(8,128)(2,1)S(1)}, bf16[8192,128]{1,0:T(8,128)(2,1)S(1)}, bf16[256,1024]{1,0:T(8,128)(2,1)S(1)}, f32[128,1024]{1,0:T(8,128)...) custom-call(bf16[256,512]{1,0:T(8,128)(2,1)} %q_hbm.1, bf16[256,128]{1,0:T(8,128)(2,1)} %k_ref.1, ...), custom_call_target="tpu_custom_call" | custom-call | tf_op jit(solution)/shard_map/pallas_call | solution.py:564
  23.8 5.7 %shard_map.47 = f32[256,512]{1,0:T(8,128)} custom-call(s32[64,64]{1,0:T(8,128)} %mask_hbm.3, bf16[256,1024]{1,0:T(8,128)(2,1)S(1)} %get-tuple-element.11.turned, f32[128,1024]{1,0:T(8,128)S(1)} %get-tuple-element.12.old_total, f32[1,1024]{1,0:T(1,128)S(1)} %get-tuple-element.13.old_mass, f32[1,1024]{1,0:T(1,128)S(1)} %get-tuple-element.14.old_top, ...), custom_call_target="tpu_custom_call" | custom-call | tf_op jit(solution)/shard_map/pallas_call | solution.py:591

commit v2 on v1

--- a/solution.py
+++ b/solution.py
@@ -208,10 +208,13 @@
         here = pl.ds(own * part, part)
         for h in range(H):
             at = slice(own * width + h * part, own * width + (h + 1) * part)
-            held[here, h * DH : (h + 1) * DH] = (total[:, at] / mass[:, at]).T
-        copy = pltpu.make_async_copy(held.at[here, :], out_ref.at[here, :], sent.at[own])
-        copy.start()
-        copies.append(copy)
+            there = pl.ds(h * DH, DH)
+            held[here, there] = (total[:, at] / mass[:, at]).T
+            copy = pltpu.make_async_copy(
+                held.at[here, there], out_ref.at[here, there], sent.at[own * H + h]
+            )
+            copy.start()
+            copies.append(copy)
     for copy in copies:
         copy.wait()
 
@@ -598,7 +601,7 @@
             pltpu.SMEM((parts, block_mask.shape[1]), jnp.int32),
             *[pltpu.VMEM(s.shape, s.dtype) for s in sums],
             pltpu.VMEM(queries.shape, jnp.float32),
-            pltpu.SemaphoreType.DMA((parts,)),
+            pltpu.SemaphoreType.DMA((parts * H,)),
             pltpu.SemaphoreType.DMA((1,)),
         ],
         compiler_params=pltpu.CompilerParams(vmem_limit_bytes=48 * 2**20),

time: 30 us -> 30 us (level)
  no operation moved by 1% of the time
where the time goes in v2:
time: 30 us; the launch traced here: 29.5 us
  Pallas kernels  29.5 us (98%)
    pallas_call x1, Pallas kernels, gathered(): pl.pallas_call(spread, out_shape=(full, full) + state, in_specs=[pl.Block...  23.8 us
    pallas_call x1, Pallas kernels, shards(): pl.pallas_call(functools.partial(attend, early), out_shape=jax.ShapeDtype...  5.68 us

profile of v2, /device:TPU:29, one launch (start us, length us, event | category | flops | bytes accessed | tf_op | source)
XLA Modules:
  0.0 29.5 jit_solution(3496862196260138817)
XLA Ops:
  0.0 23.8 %shard_map.46 = (bf16[8192,128]{1,0:T(8,128)(2,1)S(1)}, bf16[8192,128]{1,0:T(8,128)(2,1)S(1)}, bf16[256,1024]{1,0:T(8,128)(2,1)S(1)}, f32[128,1024]{1,0:T(8,128)...) custom-call(bf16[256,512]{1,0:T(8,128)(2,1)} %q_hbm.1, bf16[256,128]{1,0:T(8,128)(2,1)} %k_ref.1, ...), custom_call_target="tpu_custom_call" | custom-call | tf_op jit(solution)/shard_map/pallas_call | solution.py:567
  23.8 5.7 %shard_map.47 = f32[256,512]{1,0:T(8,128)} custom-call(s32[64,64]{1,0:T(8,128)} %mask_hbm.3, bf16[256,1024]{1,0:T(8,128)(2,1)S(1)} %get-tuple-element.11.turned, f32[128,1024]{1,0:T(8,128)S(1)} %get-tuple-element.12.old_total, f32[1,1024]{1,0:T(1,128)S(1)} %get-tuple-element.13.old_mass, f32[1,1024]{1,0:T(1,128)S(1)} %get-tuple-element.14.old_top, ...), custom_call_target="tpu_custom_call" | custom-call | tf_op jit(solution)/shard_map/pallas_call | solution.py:594
